TPU v7x, 128 devices: a whole 4x4x4 slice. The times are simulated.
128 devices in a mesh: grp: 16 (over y_hi, z, core), tp: 8 (over y_lo, x).
Axes of the slice: x: 4, y: 4 (y_hi: 2, y_lo: 2; y = y_hi * 2 + y_lo), z: 4, core: 2. Of those that a mesh axis runs over, the one named last changes fastest.
Arguments:
- tokens: bfloat16 [16384, 8192], P('grp'), may hold values from -12 to 12
- joined_weight: bfloat16 [8192, 10240], P(('grp', 'tp')), may hold values from -1.14904852 to 1.14904852
- rollout_lengths: int32 [128], P('grp'), may hold values from 1 to 128
- prompt_of: int32 [128, 1], P('grp'), may hold values from 0 to 15
- score_weight: bfloat16 [8192], P('tp'), may hold values from -0.52734375 to 0.52734375
Outputs:
- attention: bfloat16 [16384, 8192], P('grp', 'tp')
- advantages: float32 [128], P('grp')
All inputs are finite; a program needn't handle non-finite values.
Results may differ from a plain program's by a relative error of at most 0.012.
The roundings to bfloat16 on the way count: a program that leaves them out, or rounds other values in their place, can miss the bound.
Values may be sent and summed in bfloat16 or wider, within the bound.
No kernel may reach another device: no remote copies, remote signals or barrier semaphores. Data moves between devices by JAX's collectives and lax.ppermute only.
A program may use at most 128 MiB of HBM per device.

v0:
```python
import jax
import jax.numpy as jnp
from jax import lax
from jax.sharding import PartitionSpec as P

QUERY_HEADS = 64
KV_HEAD_COUNT = 8
HEAD_SIZE = 128


def copy_for_each(shard, axis):
    copies = jnp.broadcast_to(shard, (lax.axis_size(axis), *shard.shape))
    return lax.all_to_all(copies, axis, split_axis=0, concat_axis=0, tiled=True)


def taken_together(shard, axis):
    return copy_for_each(shard, axis).sum(axis=0)


def together(arrays, axis):
    ends = [0]
    for a in arrays:
        ends.append(ends[-1] + a.size)
    running = taken_together(jnp.concatenate([a.ravel() for a in arrays]), axis)
    return tuple((running[b:e].reshape(a.shape) for a, b, e in zip(arrays, ends, ends[1:])))


def project_rows(block_rows, tokens):
    return jnp.dot(tokens, block_rows, preferred_element_type=jnp.float32)


def attend(joined_matrix, rollout_length_list):
    head_ratio = QUERY_HEADS // KV_HEAD_COUNT
    slot_index = joined_matrix.shape[0] // rollout_length_list.shape[0]
    groups = joined_matrix.shape[1] // ((head_ratio + 2) * HEAD_SIZE)
    reshaped_tensor = joined_matrix.reshape(
        rollout_length_list.shape[0], slot_index, groups, head_ratio + 2, HEAD_SIZE
    )
    queries = reshaped_tensor[:, :, :, :head_ratio, :]
    key_heads = reshaped_tensor[:, :, :, head_ratio, :]
    value_heads = reshaped_tensor[:, :, :, head_ratio + 1, :]
    scores = jnp.einsum(
        "rsgah,rtgh->rgast", queries, key_heads, preferred_element_type=jnp.float32
    ) * HEAD_SIZE ** (-0.5)
    positions = jnp.arange(slot_index)
    allowed = (positions[None, None, :] <= positions[None, :, None]) & (
        positions[None, None, :] < rollout_length_list[:, None, None]
    )
    scores = jnp.where(allowed[:, None, None], scores, jnp.float32(-1e30))
    peak = jnp.max(scores, axis=-1, keepdims=True)
    expo = jnp.exp(scores - peak)
    probs = (expo / jnp.sum(expo, axis=-1, keepdims=True)).astype(jnp.bfloat16)
    mixed = jnp.einsum("rgast,rtgh->rsgah", probs, value_heads, preferred_element_type=jnp.float32)
    return mixed.reshape(joined_matrix.shape[0], groups * head_ratio * HEAD_SIZE).astype(
        jnp.bfloat16
    )


def shards(tokens, joined_weight, rollout_lengths, prompt_of, score_weight):
    grp_count = lax.axis_size("grp")
    column_block = lax.all_to_all(joined_weight, "tp", split_axis=1, concat_axis=0, tiled=True)
    joined_matrix = project_rows(lax.all_gather(column_block, "grp", axis=0, tiled=True), tokens)
    attention = attend(joined_matrix.astype(jnp.bfloat16), rollout_lengths)
    partial_value = jnp.dot(attention, score_weight, preferred_element_type=jnp.float32)
    rollouts = rollout_lengths.shape[0]
    slot_index = tokens.shape[0] // rollouts
    valid = jnp.arange(slot_index)[None, :] < rollout_lengths[:, None]
    divisor_len = rollout_lengths.astype(jnp.float32)
    local_reward = (
        jnp.sum(
            jnp.where(valid, partial_value.reshape(rollouts, slot_index), jnp.float32(0.0)), axis=1
        )
        / divisor_len
    )
    rewards = taken_together(local_reward, "tp")
    onehot = (prompt_of == jnp.arange(grp_count)[None, :]).astype(jnp.float32)
    counts, totals, squares = together(
        (
            jnp.sum(onehot, axis=0),
            jnp.sum(onehot * rewards[:, None], axis=0),
            jnp.sum(onehot * (rewards * rewards)[:, None], axis=0),
        ),
        "grp",
    )
    divisor = jnp.maximum(counts, 1.0)
    average = totals / divisor
    spread = squares / divisor - average * average
    own_mean = jnp.sum(onehot * average[None, :], axis=1)
    own_var = jnp.sum(onehot * spread[None, :], axis=1)
    advantages = (rewards - own_mean) / jnp.sqrt(own_var + 0.25)
    return (attention, advantages)


def solution(mesh):
    return jax.shard_map(
        shards,
        mesh=mesh,
        in_specs=(P("grp", None), P(("grp", "tp"), None), P("grp"), P("grp", None), P("tp")),
        out_specs=(P("grp", "tp"), P("grp")),
        check_vma=False,
    )
```

profile of v0, /device:TPU:1, one launch (start us, length us, event | category | flops | bytes accessed | tf_op | source)
XLA Modules:
  0.0 233.0 jit_solution(10680021031263918509)
XLA Ops:
  7.2 0.0 copy-start
  7.2 0.0 copy-start.2
  7.2 0.0 all-gather.2.cloned.1.call-start
  7.2 1.4 copy.62
  8.6 23.4 %all_to_all.31 = bf16[64,8,1280]{2,0,1:T(8,128)(2,1)} all-to-all(bf16[64,8,1280]{2,0,1:T(8,128)(2,1)S(1)} %bitcast.80), channel_id=1, replica_groups=mesh['grp'=16,'tp'=8] {'tp'}, dimensions={1} | all-to-all | bytes 2621440 | tf_op jit(solution)/shard_map/all_to_all | solution.py:61
  32.1 0.0 all-gather.2.cloned.1.call-update
  32.1 0.0 copy-done
  32.1 0.0 copy-done.2
  32.2 0.1 iota_compare_fusion.2
  32.2 0.2 broadcast_and_fusion
  32.4 129.7 %all-gather.2.cloned.1.call-done = bf16[8192,1280]{1,0:T(8,128)(2,1)} async-done(((bf16[512,1280]{1,0:T(8,128)(2,1)}), bf16[8192,1280]{1,0:T(8,128)(2,1)}) %all-gather.2.cloned.1.call-update) | async-done | bytes 20971536 | tf_op jit(solution)/shard_map/all_gather | solution.py:62
  162.1 28.0 %convolution_convert_fusion = bf16[1024,1280]{1,0:T(8,128)(2,1)} fusion(bf16[1024,8192]{1,0:T(8,128)(2,1)} %param.5, bf16[8192,1280]{1,0:T(8,128)(2,1)} %all-gather.2.cloned.1.call-done), kind=kOutput, calls=%fused_computation.3 | convolution fusion | flops 21476147200 | bytes 40370176 | tf_op jit(solution)/shard_map/dot_general | solution.py:29
  190.1 3.0 %copy.39 = bf16[1024,1280]{0,1:T(8,128)(2,1)S(1)} copy(bf16[1024,1280]{1,0:T(8,128)(2,1)} %convolution_convert_fusion) | data formatting | bytes 5242880 | tf_op jit(solution)/shard_map/convert_element_type | solution.py:63
  193.1 0.6 copy.55
  193.8 1.5 slice.26
  195.3 0.2 copy.52
  195.5 3.3 %copy.53 = bf16[8,128,1,8,128]{4,1,3,0,2:T(8,128)(2,1)S(1)} copy(bf16[8,128,1,8,128]{1,0,4,3,2:T(8,128)(2,1)} %slice.26) | data formatting | bytes 4194304
  198.8 0.8 fusion.1
  199.6 1.2 fusion
  200.8 0.0 copy-start.1
  200.8 1.5 fusion.10
  202.4 0.4 fusion.17
  202.8 0.2 select_reduce_fusion.4
  203.0 8.8 %all_to_all.32 = f32[8,1,8]{2,1,0:T(1,128)S(1)} all-to-all(f32[8,1,8]{2,1,0:T(1,128)S(1)} %broadcast_in_dim.23), channel_id=1, replica_groups=mesh['grp'=16,'tp'=8] {'tp'}, dimensions={0} | all-to-all | bytes 512 | tf_op jit(solution)/shard_map/all_to_all | solution.py:13
  211.8 0.0 copy-done.1
  211.8 0.1 convert_reduce_fusion
  211.9 0.1 pad_maximum_fusion
  212.0 0.6 broadcast_in_dim.24
  212.6 5.7 %all-to-all-start.2 = ((f32[16,1,48]{2,1,0:T(1,128)}), f32[16,1,48]{2,1,0:T(1,128)S(1)}, u32[]{:S(2)}, u32[]{:S(2)}) async-start(f32[16,1,48]{2,1,0:T(1,128)} %broadcast_in_dim.24), calls=%async_computation.2 | async-start | bytes 16384 | tf_op jit(solution)/shard_map/all_to_all | solution.py:13
  218.3 2.8 %copy.44 = bf16[8,128,1,8,128]{4,3,1,0,2:T(8,128)(2,1)} copy(bf16[8,128,1,8,128]{1,4,3,0,2:T(8,128)(2,1)S(1)} %bitcast.77) | data formatting | bytes 4194304 | tf_op jit(solution)/shard_map/convert_element_type | solution.py:54
  221.1 3.5 %copy.61 = bf16[128,8,8,128]{3,1,2,0:T(8,128)(2,1)} copy(bf16[128,8,8,128]{3,2,1,0:T(8,128)(2,1)} %bitcast.78) | data formatting | bytes 4194304
  224.7 0.7 all-to-all-done.2
  225.3 0.1 multiply_subtract_fusion
  225.4 0.2 select_reduce_fusion.1
  225.6 0.5 rsqrt_multiply_fusion
  (8 shorter events, 0.1 us)
Async XLA Ops:
  7.2 24.9 %copy-start = (bf16[1024]{0:T(1024)(128)(2,1)S(1)}, bf16[1024]{0:T(1024)(128)(2,1)}, u32[]{:S(2)}) copy-start(bf16[1024]{0:T(1024)(128)(2,1)} %param.9) | copy-start | bytes 6148
  7.2 25.0 %copy-start.2 = (s32[8]{0:T(128)S(1)}, s32[8]{0:T(128)}, u32[]{:S(2)}) copy-start(s32[8]{0:T(128)} %param.7) | copy-start | bytes 100
  7.2 155.0 %all-gather.2.cloned.1.call-start = ((), (), s32[]{:S(2)}) async-start(), calls=%async_computation.3 | async-start | bytes 22282240 | tf_op jit(solution)/shard_map/all_gather | solution.py:62
  200.8 11.0 %copy-start.1 = (s32[8,1]{0,1:T(1,128)S(1)}, s32[8,1]{0,1:T(1,128)}, u32[]{:S(2)}) copy-start(s32[8,1]{0,1:T(1,128)} %param.8) | copy-start | bytes 100
  212.6 12.7 %all-to-all-start.2 = ((f32[16,1,48]{2,1,0:T(1,128)}), f32[16,1,48]{2,1,0:T(1,128)S(1)}, u32[]{:S(2)}, u32[]{:S(2)}) async-start(f32[16,1,48]{2,1,0:T(1,128)} %broadcast_in_dim.24), calls=%async_computation.2 | async-start | bytes 16384 | tf_op jit(solution)/shard_map/all_to_all | solution.py:13
Sparse Core Ops, SparseCore 0:
  32.2 129.8 all-gather.1
where the time goes:
time: 233 us
  waiting for transfers between devices  130 us (56%)
  blocking collectives  32.3 us (14%)
  matrix products  30.7 us (13%)
  local copies, waits for them, and re-layouts  17 us (7%)
  between operations  14.2 us (6%)
  starting transfers between devices  5.74 us (2%)
  other arithmetic  2.72 us (1%)
    all_gather x1, waiting for transfers between devices, shards(): lax.all_gather(column_block, 'grp', axis=0, tiled=True)  130 us
    dot_general x1, matrix products, project_rows(): return jnp.dot(tokens, block_rows, preferred_element_type=jnp.float32)  28 us
    all_to_all x1, blocking collectives, shards(): lax.all_to_all(joined_weight, 'tp', split_axis=1, concat_axis=0, tiled=True)  23.4 us
    all_to_all x1, blocking collectives, copy_for_each(): return lax.all_to_all(copies, axis, split_axis=0, concat_axis=0, tiled=True)  8.82 us
    unnamed x11, local copies, waits for them, and re-layouts  7.72 us
    all_to_all x1, starting transfers between devices, copy_for_each(): return lax.all_to_all(copies, axis, split_axis=0, concat_axis=0, tiled=True)  5.7 us
  transfers between devices with their start and end apart: 2, of which 2 were waited for; matrix products, arithmetic and copies ran while one was open for 3% of the time, Pallas kernels for 0%

commit v1 on v0

--- a/solution.py
+++ b/solution.py
@@ -2,6 +2,7 @@
 import jax.numpy as jnp
 from jax import lax
 from jax.sharding import PartitionSpec as P
+from jax.lax import all_to_all, psum
 
 QUERY_HEADS = 64
 KV_HEAD_COUNT = 8
@@ -57,9 +58,22 @@
 
 
 def shards(tokens, joined_weight, rollout_lengths, prompt_of, score_weight):
+
+    def _divide_sections(which_dim, field_in):
+        z1 = jnp.concatenate(
+            all_to_all(
+                jnp.stack([field_in for _ in range(psum(1, axis_name="grp"))], axis=0),
+                split_axis=0,
+                concat_axis=0,
+                axis_name="grp",
+            ),
+            axis=which_dim,
+        )
+        return z1
+
     grp_count = lax.axis_size("grp")
     column_block = lax.all_to_all(joined_weight, "tp", split_axis=1, concat_axis=0, tiled=True)
-    joined_matrix = project_rows(lax.all_gather(column_block, "grp", axis=0, tiled=True), tokens)
+    joined_matrix = project_rows(_divide_sections(0, column_block), tokens)
     attention = attend(joined_matrix.astype(jnp.bfloat16), rollout_lengths)
     partial_value = jnp.dot(attention, score_weight, preferred_element_type=jnp.float32)
     rollouts = rollout_lengths.shape[0]

time: 233 us -> 436 us (1.87)
  waiting for transfers between devices: 130 us -> 322 us
  starting transfers between devices: 5.74 us -> 23.6 us
  between operations: 14.2 us -> 0.77 us
  local copies, waits for them, and re-layouts: 17 us -> 24.4 us
    all_to_all x0 -> x1, waiting for transfers between devices: none -> 322 us  [_divide_sections(): all_to_all(jnp.stack([field_in for _ in range(psum(1, axis_name='grp'))],...]
    all_gather x1 -> x0, waiting for transfers between devices: 130 us -> none  [shards(): lax.all_gather(column_block, 'grp', axis=0, tiled=True)]
    all_to_all x0 -> x1, starting transfers between devices: none -> 9.58 us  [_divide_sections(): all_to_all(jnp.stack([field_in for _ in range(psum(1, axis_name='grp'))],...]
    all_to_all x1, starting transfers between devices: 5.7 us -> 14 us  [copy_for_each(): return lax.all_to_all(copies, axis, split_axis=0, concat_axis=0, tiled=True)]
    another operation x0 -> x1, local copies, waits for them, and re-layouts: none -> 7.41 us  [_divide_sections(): jnp.stack([field_in for _ in range(psum(1, axis_name='grp'))], axis=0)]
  transfers between devices with their start and end apart: 2 -> 2, of which waited for: 2 -> 2; matrix products, arithmetic and copies ran while one was open for 3% -> 2% of each run, Pallas kernels for 0% -> 0%
where the time goes in v1:
time: 436 us; the launch traced here: 435 us
  waiting for transfers between devices  322 us (74%)
  blocking collectives  30.7 us (7%)
  matrix products  30.7 us (7%)
  local copies, waits for them, and re-layouts  24.4 us (6%)
  starting transfers between devices  23.6 us (5%)
    all_to_all x1, waiting for transfers between devices, _divide_sections(): all_to_all(jnp.stack([field_in for _ in range(psum(1, axis_name='grp'))],...  322 us
    dot_general x1, matrix products, project_rows(): return jnp.dot(tokens, block_rows, preferred_element_type=jnp.float32)  28 us
    all_to_all x1, blocking collectives, shards(): lax.all_to_all(joined_weight, 'tp', split_axis=1, concat_axis=0, tiled=True)  23.3 us
    all_to_all x1, starting transfers between devices, copy_for_each(): return lax.all_to_all(copies, axis, split_axis=0, concat_axis=0, tiled=True)  14 us
    all_to_all x1, starting transfers between devices, _divide_sections(): all_to_all(jnp.stack([field_in for _ in range(psum(1, axis_name='grp'))],...  9.58 us
  transfers between devices with their start and end apart: 2, of which 2 were waited for; matrix products, arithmetic and copies ran while one was open for 2% of the time, Pallas kernels for 0%

profile of v1, /device:TPU:1, one launch (start us, length us, event | category | flops | bytes accessed | tf_op | source)
XLA Modules:
  0.0 435.4 jit_solution(9763222292497925639)
XLA Ops:
  0.6 1.4 copy.62
  2.0 23.3 %all_to_all.33 = bf16[64,8,1280]{2,0,1:T(8,128)(2,1)S(1)} all-to-all(bf16[64,8,1280]{2,0,1:T(8,128)(2,1)S(1)} %bitcast.80), channel_id=1, replica_groups=mesh['grp'=16,'tp'=8] {'tp'}, dimensions={1} | all-to-all | bytes 2621440 | tf_op jit(solution)/shard_map/all_to_all | solution.py:75
  25.4 7.4 %stack.5 = bf16[16,512,1280]{2,1,0:T(8,128)(2,1)} broadcast(bf16[512,1280]{1,0:T(8,128)(2,1)S(1)} %bitcast.81), dimensions={1,2} | broadcast | bytes 22282240 | tf_op jit(solution)/shard_map/stack | solution.py:65
  32.8 0.0 copy-start
  32.8 0.0 copy-start.2
  32.8 9.6 %all-to-all-start.1 = ((bf16[16,512,1280]{2,1,0:T(8,128)(2,1)}), bf16[16,512,1280]{2,1,0:T(8,128)(2,1)}, u32[]{:S(2)}, u32[]{:S(2)}) async-start(bf16[16,512,1280]{2,1,0:T(8,128)(2,1)} %stack.5), calls=%async_computation.1 | async-start | bytes 41943040 | tf_op jit(solution)/shard_map/all_to_all | solution.py:64
  42.4 0.0 copy-done
  42.4 0.0 copy-done.2
  42.4 0.1 iota_compare_fusion.2
  42.5 0.2 broadcast_and_fusion
  42.7 321.8 %all-to-all-done.1 = bf16[16,512,1280]{2,1,0:T(8,128)(2,1)} async-done(((bf16[16,512,1280]{2,1,0:T(8,128)(2,1)}), bf16[16,512,1280]{2,1,0:T(8,128)(2,1)}, u32[]{:S(2)}, u32[]{:S(2)}) %all-to-all-start.1) | async-done | bytes 20971552 | tf_op jit(solution)/shard_map/all_to_all | solution.py:64
  364.5 28.0 %convolution_convert_fusion = bf16[1024,1280]{1,0:T(8,128)(2,1)} fusion(bf16[1024,8192]{1,0:T(8,128)(2,1)} %param.5, bf16[8192,1280]{1,0:T(8,128)(2,1)} %bitcast.2), kind=kOutput, calls=%fused_computation.3 | convolution fusion | flops 21476147200 | bytes 40370176 | tf_op jit(solution)/shard_map/dot_general | solution.py:30
  392.5 3.0 copy.39
  395.5 0.6 copy.55
  396.2 1.5 slice.26
  397.6 0.2 copy.52
  397.9 3.3 copy.53
  401.2 0.8 fusion.1
  402.0 1.2 fusion
  403.2 0.0 copy-start.1
  403.2 1.5 fusion.10
  404.8 0.4 fusion.17
  405.1 0.2 select_reduce_fusion.4
  405.3 7.4 %all_to_all.34 = f32[8,1,8]{2,1,0:T(1,128)S(1)} all-to-all(f32[8,1,8]{2,1,0:T(1,128)S(1)} %broadcast_in_dim.23), channel_id=1, replica_groups=mesh['grp'=16,'tp'=8] {'tp'}, dimensions={0} | all-to-all | bytes 512 | tf_op jit(solution)/shard_map/all_to_all | solution.py:14
  412.8 0.0 copy-done.1
  412.8 0.1 convert_reduce_fusion
  412.9 0.1 pad_maximum_fusion
  412.9 0.6 broadcast_in_dim.24
  413.6 14.0 %all-to-all-start.3 = ((f32[16,1,48]{2,1,0:T(1,128)}), f32[16,1,48]{2,1,0:T(1,128)S(1)}, u32[]{:S(2)}, u32[]{:S(2)}) async-start(f32[16,1,48]{2,1,0:T(1,128)} %broadcast_in_dim.24), calls=%async_computation.3 | async-start | bytes 16384 | tf_op jit(solution)/shard_map/all_to_all | solution.py:14
  427.5 2.8 copy.44
  430.3 3.5 copy.61
  433.9 0.7 all-to-all-done.3
  434.6 0.1 multiply_subtract_fusion
  434.6 0.2 select_reduce_fusion.1
  434.8 0.5 rsqrt_multiply_fusion
  (8 shorter events, 0.1 us)
Async XLA Ops:
  32.8 9.6 %copy-start = (bf16[1024]{0:T(1024)(128)(2,1)S(1)}, bf16[1024]{0:T(1024)(128)(2,1)}, u32[]{:S(2)}) copy-start(bf16[1024]{0:T(1024)(128)(2,1)} %param.9) | copy-start | bytes 6148
  32.8 9.6 %copy-start.2 = (s32[8]{0:T(128)S(1)}, s32[8]{0:T(128)}, u32[]{:S(2)}) copy-start(s32[8]{0:T(128)} %param.7) | copy-start | bytes 100
  32.8 331.7 %all-to-all-start.1 = ((bf16[16,512,1280]{2,1,0:T(8,128)(2,1)}), bf16[16,512,1280]{2,1,0:T(8,128)(2,1)}, u32[]{:S(2)}, u32[]{:S(2)}) async-start(bf16[16,512,1280]{2,1,0:T(8,128)(2,1)} %stack.5), calls=%async_computation.1 | async-start | bytes 41943040 | tf_op jit(solution)/shard_map/all_to_all | solution.py:64
  403.2 9.6 %copy-start.1 = (s32[8,1]{0,1:T(1,128)S(1)}, s32[8,1]{0,1:T(1,128)}, u32[]{:S(2)}) copy-start(s32[8,1]{0,1:T(1,128)} %param.8) | copy-start | bytes 100
  413.6 21.0 %all-to-all-start.3 = ((f32[16,1,48]{2,1,0:T(1,128)}), f32[16,1,48]{2,1,0:T(1,128)S(1)}, u32[]{:S(2)}, u32[]{:S(2)}) async-start(f32[16,1,48]{2,1,0:T(1,128)} %broadcast_in_dim.24), calls=%async_computation.3 | async-start | bytes 16384 | tf_op jit(solution)/shard_map/all_to_all | solution.py:14
